TPU v7x, 32 devices: a whole 2x2x4 slice. The times are simulated.
32 devices in a mesh: row: 4 (over z), col: 8 (over y, x, core).
Axes of the slice: x: 2, y: 2, z: 4, core: 2. Of those that a mesh axis runs over, the one named last changes fastest.
Arguments:
- rhs: float32 [64, 131072], P(None, ('row', 'col')), may hold values from -6 to 6
- pivots: int32 [4096], replicated, may hold values from 0 to 131071, as said below
- factor: float32 [4096, 4, 8, 128], P('row', None, 'col'), as said below
- diag_inv: float32 [8, 512, 512], P('row'), as said below
Outputs:
- solution: float32 [64, 4, 8, 128], P(None, None, 'col')
Inputs may be any that keep to these rules, and one draw needn't show every extreme that they name: `pivots`: distinct column numbers, the first 4096 entries of a permutation of 0 .. 131071. `factor`: entry (row i, column q) is zero where q >= 512 * (i // 512). `diag_inv`: each block is unit lower triangular.
All inputs are finite; a program needn't handle non-finite values.
Results may differ from a plain program's by a relative error of at most 0.0001.
Values sent between devices are 32-bit elements; how exact they have to be, the bound alone decides.
A program may use at most 64 MiB of HBM per device.

v0:
```python
import jax
import jax.numpy as jnp
from jax import lax
from jax.sharding import PartitionSpec as P


def broadcast(shard, axis, root):
    mine = lax.axis_index(axis) == root
    return lax.psum(jnp.where(mine, shard, jnp.zeros_like(shard)), axis)


def apply_inverse(values, block_inv):
    return lax.dot_general(
        values,
        block_inv,
        (((1,), (1,)), ((), ())),
        precision=lax.Precision.HIGHEST,
        preferred_element_type=jnp.float32,
    )


def per_device(rhs, pivots, factor, diag_inv):
    my_row = lax.axis_index("row")
    my_col = lax.axis_index("col")
    col_count = lax.axis_size("col")
    rhs_count = rhs.shape[0]
    slab_rows = factor.shape[0]
    rounds = factor.shape[1]
    piece_len = factor.shape[3]
    block_len = diag_inv.shape[1]
    pieces = block_len // piece_len
    blocks_here = slab_rows // block_len
    total_blocks = blocks_here * lax.axis_size("row")
    first_column = (my_row * col_count + my_col) * rhs.shape[1]
    source_len = rhs.shape[1]
    located = pivots - first_column
    inside = (located >= 0) & (located < source_len)
    taken = jnp.take(rhs, jnp.clip(located, 0, source_len - 1), axis=1)
    taken = jnp.where(inside[None, :], taken, 0.0)
    permuted = lax.psum_scatter(
        jnp.transpose(
            taken.reshape(rhs_count, blocks_here * lax.axis_size("row"), block_len), (1, 0, 2)
        ),
        "row",
        scatter_dimension=0,
        tiled=True,
    )
    permuted = lax.psum(permuted, "col")
    factor_rows = factor.reshape(slab_rows, rounds * piece_len)

    def advance(number, solved):
        owner_row = number // blocks_here
        local_block = number % blocks_here
        block_rows = lax.dynamic_slice_in_dim(factor_rows, local_block * block_len, block_len, 0)
        partial_value = lax.dot_general(
            solved.reshape(rhs_count, rounds * piece_len),
            block_rows,
            (((1,), (1,)), ((), ())),
            precision=lax.Precision.HIGHEST,
            preferred_element_type=jnp.float32,
        )
        own_rhs = lax.dynamic_index_in_dim(permuted, local_block, 0, keepdims=False)
        block_inv = lax.dynamic_index_in_dim(diag_inv, local_block, 0, keepdims=False)
        summed = lax.psum(partial_value, "col")
        fresh = apply_inverse(own_rhs - summed, block_inv)
        fresh = broadcast(fresh, "row", owner_row)
        first_piece = number * pieces
        offset_piece = (my_col - first_piece) % col_count
        owns = offset_piece < pieces
        which = jnp.clip(offset_piece, 0, pieces - 1)
        local_round = jnp.clip((first_piece + offset_piece) // col_count, 0, rounds - 1)
        piece = lax.dynamic_slice_in_dim(fresh, which * piece_len, piece_len, 1)
        updated = lax.dynamic_update_index_in_dim(solved, piece[:, None, :], local_round, 1)
        return jnp.where(owns, updated, solved)

    start_state = jnp.zeros((rhs_count, rounds, 1, piece_len), jnp.float32)
    return lax.fori_loop(0, total_blocks, advance, start_state)


def solution(mesh):
    return jax.shard_map(
        per_device,
        mesh=mesh,
        in_specs=(P(None, ("row", "col")), P(), P("row", None, "col", None), P("row", None, None)),
        out_specs=P(None, None, "col", None),
        check_vma=False,
    )
```

profile of v0, /device:TPU:0, one launch (start us, length us, event | category | flops | bytes accessed | tf_op | source)
XLA Modules:
  0.0 882.2 jit_solution(17491685887215917001)
XLA Ops:
  8.1 1.8 copy.8
  9.9 14.1 %gather_fusion = f32[4096,64]{1,0:T(8,128)} fusion(f32[64,4096]{0,1:T(8,128)S(1)} %copy.8, s32[4096]{0:T(1024)S(1)} %fusion.8), kind=kCustom, calls=%fused_computation | custom fusion | bytes 2113536 | tf_op jit(solution)/shard_map/jit(_take)/gather | solution.py:38
  24.0 2.2 copy.9
  27.4 30.1 %reduce-scatter.2.cloned.1.call-done = f32[2,64,512]{2,1,0:T(8,128)} async-done(((f32[8,64,512]{2,1,0:T(8,128)}), f32[2,64,512]{2,1,0:T(8,128)}) %reduce-scatter.2.cloned.1.call-update) | async-done | bytes 262160 | tf_op jit(solution)/shard_map/reduce_scatter | solution.py:40
  59.3 53.7 %all-reduce.4.cloned.1.call-done = f32[2,64,512]{2,1,0:T(8,128)} async-done(((f32[2,64,512]{2,1,0:T(8,128)}), f32[2,64,512]{2,1,0:T(8,128)}) %all-reduce.4.cloned.1.call-update) | async-done | bytes 262160 | tf_op jit(solution)/shard_map/psum | solution.py:48
  113.0 761.7 %while.16 = (s32[]{:T(128)}, f32[64,4,1,128]{3,1,0,2:T(4,128)S(1)}, s32[]{:T(128)}, f32[2,64,512]{2,1,0:T(8,128)}, f32[1024,512]{1,0:T(8,128)S(1)}, /*index=5*/f...) while((s32[]{:T(128)}, f32[64,4,1,128]{3,1,0,2:T(4,128)S(1)}, ...), condition=%wide.region_5.6_spmd, body=%wide.region_2.5_spmd.sunk | while | flops 402792448 | bytes 4557184 | solution.py:77
  115.0 54.8 %all-reduce.6.cloned.1.call-done = f32[64,512]{1,0:T(8,128)} async-done(((f32[64,512]{1,0:T(8,128)}), f32[64,512]{1,0:T(8,128)}) %all-reduce.6.cloned.1.call-update) | async-done | bytes 131088 | tf_op jit(solution)/shard_map/while/body/eval_jaxpr/psum | solution.py:64
  169.7 3.1 convolution_select_fusion.2
  172.9 34.1 %all-reduce.8.cloned.1.call-done = f32[64,512]{1,0:T(8,128)} async-done(((f32[64,512]{1,0:T(8,128)}), f32[64,512]{1,0:T(8,128)}) %all-reduce.8.cloned.1.call-update) | async-done | bytes 131088 | tf_op jit(solution)/shard_map/while/body/eval_jaxpr/psum | solution.py:9
  208.1 1.8 convolution_bitcast_fusion.2
  210.0 54.8 %all-reduce.6.cloned.1.call-done = f32[64,512]{1,0:T(8,128)} async-done(((f32[64,512]{1,0:T(8,128)}), f32[64,512]{1,0:T(8,128)}) %all-reduce.6.cloned.1.call-update) | async-done | bytes 131088 | tf_op jit(solution)/shard_map/while/body/eval_jaxpr/psum | solution.py:64
  264.8 3.1 convolution_select_fusion.2
  268.0 34.1 %all-reduce.8.cloned.1.call-done = f32[64,512]{1,0:T(8,128)} async-done(((f32[64,512]{1,0:T(8,128)}), f32[64,512]{1,0:T(8,128)}) %all-reduce.8.cloned.1.call-update) | async-done | bytes 131088 | tf_op jit(solution)/shard_map/while/body/eval_jaxpr/psum | solution.py:9
  305.1 55.1 %all-reduce.6.cloned.1.call-done = f32[64,512]{1,0:T(8,128)} async-done(((f32[64,512]{1,0:T(8,128)}), f32[64,512]{1,0:T(8,128)}) %all-reduce.6.cloned.1.call-update) | async-done | bytes 131088 | tf_op jit(solution)/shard_map/while/body/eval_jaxpr/psum | solution.py:64
  360.1 3.1 convolution_select_fusion.2
  363.3 34.1 %all-reduce.8.cloned.1.call-done = f32[64,512]{1,0:T(8,128)} async-done(((f32[64,512]{1,0:T(8,128)}), f32[64,512]{1,0:T(8,128)}) %all-reduce.8.cloned.1.call-update) | async-done | bytes 131088 | tf_op jit(solution)/shard_map/while/body/eval_jaxpr/psum | solution.py:9
  400.4 55.1 %all-reduce.6.cloned.1.call-done = f32[64,512]{1,0:T(8,128)} async-done(((f32[64,512]{1,0:T(8,128)}), f32[64,512]{1,0:T(8,128)}) %all-reduce.6.cloned.1.call-update) | async-done | bytes 131088 | tf_op jit(solution)/shard_map/while/body/eval_jaxpr/psum | solution.py:64
  455.5 3.1 convolution_select_fusion.2
  458.7 34.1 %all-reduce.8.cloned.1.call-done = f32[64,512]{1,0:T(8,128)} async-done(((f32[64,512]{1,0:T(8,128)}), f32[64,512]{1,0:T(8,128)}) %all-reduce.8.cloned.1.call-update) | async-done | bytes 131088 | tf_op jit(solution)/shard_map/while/body/eval_jaxpr/psum | solution.py:9
  495.8 55.1 %all-reduce.6.cloned.1.call-done = f32[64,512]{1,0:T(8,128)} async-done(((f32[64,512]{1,0:T(8,128)}), f32[64,512]{1,0:T(8,128)}) %all-reduce.6.cloned.1.call-update) | async-done | bytes 131088 | tf_op jit(solution)/shard_map/while/body/eval_jaxpr/psum | solution.py:64
  550.9 3.1 convolution_select_fusion.2
  554.1 34.1 %all-reduce.8.cloned.1.call-done = f32[64,512]{1,0:T(8,128)} async-done(((f32[64,512]{1,0:T(8,128)}), f32[64,512]{1,0:T(8,128)}) %all-reduce.8.cloned.1.call-update) | async-done | bytes 131088 | tf_op jit(solution)/shard_map/while/body/eval_jaxpr/psum | solution.py:9
  589.3 1.8 convolution_bitcast_fusion.2
  591.1 55.1 %all-reduce.6.cloned.1.call-done = f32[64,512]{1,0:T(8,128)} async-done(((f32[64,512]{1,0:T(8,128)}), f32[64,512]{1,0:T(8,128)}) %all-reduce.6.cloned.1.call-update) | async-done | bytes 131088 | tf_op jit(solution)/shard_map/while/body/eval_jaxpr/psum | solution.py:64
  646.2 3.1 convolution_select_fusion.2
  649.4 34.1 %all-reduce.8.cloned.1.call-done = f32[64,512]{1,0:T(8,128)} async-done(((f32[64,512]{1,0:T(8,128)}), f32[64,512]{1,0:T(8,128)}) %all-reduce.8.cloned.1.call-update) | async-done | bytes 131088 | tf_op jit(solution)/shard_map/while/body/eval_jaxpr/psum | solution.py:9
  686.5 54.8 %all-reduce.6.cloned.1.call-done = f32[64,512]{1,0:T(8,128)} async-done(((f32[64,512]{1,0:T(8,128)}), f32[64,512]{1,0:T(8,128)}) %all-reduce.6.cloned.1.call-update) | async-done | bytes 131088 | tf_op jit(solution)/shard_map/while/body/eval_jaxpr/psum | solution.py:64
  741.3 3.1 convolution_select_fusion.2
  744.5 34.1 %all-reduce.8.cloned.1.call-done = f32[64,512]{1,0:T(8,128)} async-done(((f32[64,512]{1,0:T(8,128)}), f32[64,512]{1,0:T(8,128)}) %all-reduce.8.cloned.1.call-update) | async-done | bytes 131088 | tf_op jit(solution)/shard_map/while/body/eval_jaxpr/psum | solution.py:9
  781.6 54.8 %all-reduce.6.cloned.1.call-done = f32[64,512]{1,0:T(8,128)} async-done(((f32[64,512]{1,0:T(8,128)}), f32[64,512]{1,0:T(8,128)}) %all-reduce.6.cloned.1.call-update) | async-done | bytes 131088 | tf_op jit(solution)/shard_map/while/body/eval_jaxpr/psum | solution.py:64
  836.3 3.1 convolution_select_fusion.2
  839.5 34.1 %all-reduce.8.cloned.1.call-done = f32[64,512]{1,0:T(8,128)} async-done(((f32[64,512]{1,0:T(8,128)}), f32[64,512]{1,0:T(8,128)}) %all-reduce.8.cloned.1.call-update) | async-done | bytes 131088 | tf_op jit(solution)/shard_map/while/body/eval_jaxpr/psum | solution.py:9
  (75 shorter events, 24.8 us)
Async XLA Ops:
  6.5 51.0 %reduce-scatter.2.cloned.1.call-start = ((), (), s32[]{:S(2)}) async-start(), calls=%async_computation.1 | async-start | bytes 1310720 | tf_op jit(solution)/shard_map/reduce_scatter | solution.py:40
  27.3 85.6 %all-reduce.4.cloned.1.call-start = ((), (), s32[]{:S(2)}) async-start(), calls=%async_computation.2 | async-start | bytes 524288 | tf_op jit(solution)/shard_map/psum | solution.py:48
  113.0 56.7 %all-reduce.6.cloned.1.call-start = ((), (), s32[]{:S(2)}) async-start(), calls=%async_computation.3 | async-start | bytes 262144 | tf_op jit(solution)/shard_map/while/body/eval_jaxpr/psum | solution.py:64
  114.9 92.2 %all-reduce.8.cloned.1.call-start = ((), (), s32[]{:S(2)}) async-start(), calls=%async_computation.4 | async-start | bytes 262144 | tf_op jit(solution)/shard_map/while/body/eval_jaxpr/psum | solution.py:9
  208.1 56.7 %all-reduce.6.cloned.1.call-start = ((), (), s32[]{:S(2)}) async-start(), calls=%async_computation.3 | async-start | bytes 262144 | tf_op jit(solution)/shard_map/while/body/eval_jaxpr/psum | solution.py:64
  209.9 92.2 %all-reduce.8.cloned.1.call-start = ((), (), s32[]{:S(2)}) async-start(), calls=%async_computation.4 | async-start | bytes 262144 | tf_op jit(solution)/shard_map/while/body/eval_jaxpr/psum | solution.py:9
  303.1 57.0 %all-reduce.6.cloned.1.call-start = ((), (), s32[]{:S(2)}) async-start(), calls=%async_computation.3 | async-start | bytes 262144 | tf_op jit(solution)/shard_map/while/body/eval_jaxpr/psum | solution.py:64
  305.0 92.5 %all-reduce.8.cloned.1.call-start = ((), (), s32[]{:S(2)}) async-start(), calls=%async_computation.4 | async-start | bytes 262144 | tf_op jit(solution)/shard_map/while/body/eval_jaxpr/psum | solution.py:9
  398.5 57.0 %all-reduce.6.cloned.1.call-start = ((), (), s32[]{:S(2)}) async-start(), calls=%async_computation.3 | async-start | bytes 262144 | tf_op jit(solution)/shard_map/while/body/eval_jaxpr/psum | solution.py:64
  400.4 92.5 %all-reduce.8.cloned.1.call-start = ((), (), s32[]{:S(2)}) async-start(), calls=%async_computation.4 | async-start | bytes 262144 | tf_op jit(solution)/shard_map/while/body/eval_jaxpr/psum | solution.py:9
  493.8 57.0 %all-reduce.6.cloned.1.call-start = ((), (), s32[]{:S(2)}) async-start(), calls=%async_computation.3 | async-start | bytes 262144 | tf_op jit(solution)/shard_map/while/body/eval_jaxpr/psum | solution.py:64
  495.7 92.5 %all-reduce.8.cloned.1.call-start = ((), (), s32[]{:S(2)}) async-start(), calls=%async_computation.4 | async-start | bytes 262144 | tf_op jit(solution)/shard_map/while/body/eval_jaxpr/psum | solution.py:9
  589.2 57.0 %all-reduce.6.cloned.1.call-start = ((), (), s32[]{:S(2)}) async-start(), calls=%async_computation.3 | async-start | bytes 262144 | tf_op jit(solution)/shard_map/while/body/eval_jaxpr/psum | solution.py:64
  591.1 92.5 %all-reduce.8.cloned.1.call-start = ((), (), s32[]{:S(2)}) async-start(), calls=%async_computation.4 | async-start | bytes 262144 | tf_op jit(solution)/shard_map/while/body/eval_jaxpr/psum | solution.py:9
  684.6 56.7 %all-reduce.6.cloned.1.call-start = ((), (), s32[]{:S(2)}) async-start(), calls=%async_computation.3 | async-start | bytes 262144 | tf_op jit(solution)/shard_map/while/body/eval_jaxpr/psum | solution.py:64
  686.4 92.2 %all-reduce.8.cloned.1.call-start = ((), (), s32[]{:S(2)}) async-start(), calls=%async_computation.4 | async-start | bytes 262144 | tf_op jit(solution)/shard_map/while/body/eval_jaxpr/psum | solution.py:9
  779.6 56.7 %all-reduce.6.cloned.1.call-start = ((), (), s32[]{:S(2)}) async-start(), calls=%async_computation.3 | async-start | bytes 262144 | tf_op jit(solution)/shard_map/while/body/eval_jaxpr/psum | solution.py:64
  781.5 92.2 %all-reduce.8.cloned.1.call-start = ((), (), s32[]{:S(2)}) async-start(), calls=%async_computation.4 | async-start | bytes 262144 | tf_op jit(solution)/shard_map/while/body/eval_jaxpr/psum | solution.py:9
  874.7 0.7 copy-start
Sparse Core Ops, SparseCore 0:
  27.5 29.9 reduce-scatter.1
  60.5 52.3 all-reduce.3
  116.8 52.8 all-reduce.5
  173.0 34.0 all-reduce.7
  211.6 53.1 all-reduce.5
  268.0 34.0 all-reduce.7
  307.0 53.1 all-reduce.5
  363.4 34.0 all-reduce.7
  402.3 53.1 all-reduce.5
  458.8 34.0 all-reduce.7
  497.7 53.1 all-reduce.5
  554.1 34.0 all-reduce.7
  593.0 53.1 all-reduce.5
  649.5 34.0 all-reduce.7
  688.1 53.1 all-reduce.5
  744.6 34.0 all-reduce.7
  783.2 53.1 all-reduce.5
  839.6 34.0 all-reduce.7
where the time goes:
time: 883 us; the launch traced here: 882 us
  waiting for transfers between devices  796 us (90%)
  matrix products  39.5 us (4%)
  local copies, waits for them, and re-layouts  28 us (3%)
  between operations  13.5 us (2%)
    psum x8, waiting for transfers between devices, advance(): summed = lax.psum(partial_value, 'col')  439 us
    psum x8, waiting for transfers between devices, broadcast(): return lax.psum(jnp.where(mine, shard, jnp.zeros_like(shard)), axis)  273 us
    psum x1, waiting for transfers between devices, per_device(): permuted = lax.psum(permuted, 'col')  53.7 us
    reduce_scatter x1, waiting for transfers between devices, per_device(): lax.psum_scatter(jnp.transpose(taken.reshape(rhs_count, blocks_here * lax...  30.1 us
    dot_general x8, matrix products, apply_inverse(): lax.dot_general(values, block_inv, (((1,), (1,)), ((), ())), precision=la...  25.1 us
  transfers between devices with their start and end apart: 18, of which 18 were waited for; matrix products, arithmetic and copies ran while one was open for 0% of the time, Pallas kernels for 0%

commit v1 on v0

--- a/solution.py
+++ b/solution.py
@@ -2,6 +2,14 @@
 import jax.numpy as jnp
 from jax import lax
 from jax.sharding import PartitionSpec as P
+
+
+def add_in_pairs(block, mesh_axis):
+    count, total = (lax.axis_size(mesh_axis), block)
+    for stride in [1 << k for k in range(count.bit_length() - 1)]:
+        route = [(i, i ^ stride) for i in range(count)]
+        total = total + lax.ppermute(total, mesh_axis, route)
+    return total
 
 
 def broadcast(shard, axis, root):
@@ -45,7 +53,7 @@
         scatter_dimension=0,
         tiled=True,
     )
-    permuted = lax.psum(permuted, "col")
+    permuted = add_in_pairs(permuted, "col")
     factor_rows = factor.reshape(slab_rows, rounds * piece_len)
 
     def advance(number, solved):

time: 883 us -> 844 us (0.956)
  waiting for transfers between devices: 796 us -> 754 us
    psum x1 -> x0, waiting for transfers between devices: 53.7 us -> none  [per_device(): permuted = lax.psum(permuted, 'col')]
    ppermute x0 -> x3, waiting for transfers between devices: none -> 12.8 us  [add_in_pairs(): total = total + lax.ppermute(total, mesh_axis, route)]
  transfers between devices with their start and end apart: 18 -> 20, of which waited for: 18 -> 20; matrix products, arithmetic and copies ran while one was open for 0% -> 0% of each run, Pallas kernels for 0% -> 0%
where the time goes in v1:
time: 844 us; the launch traced here: 843 us
  waiting for transfers between devices  754 us (89%)
  matrix products  39 us (5%)
  local copies, waits for them, and re-layouts  28.1 us (3%)
  between operations  13.2 us (2%)
    psum x8, waiting for transfers between devices, advance(): summed = lax.psum(partial_value, 'col')  437 us
    psum x8, waiting for transfers between devices, broadcast(): return lax.psum(jnp.where(mine, shard, jnp.zeros_like(shard)), axis)  273 us
    reduce_scatter x1, waiting for transfers between devices, per_device(): lax.psum_scatter(jnp.transpose(taken.reshape(rhs_count, blocks_here * lax...  30.2 us
    dot_general x8, matrix products, apply_inverse(): lax.dot_general(values, block_inv, (((1,), (1,)), ((), ())), precision=la...  24.5 us
  transfers between devices with their start and end apart: 20, of which 20 were waited for; matrix products, arithmetic and copies ran while one was open for 0% of the time, Pallas kernels for 0%

profile of v1, /device:TPU:0, one launch (start us, length us, event | category | flops | bytes accessed | tf_op | source)
XLA Modules:
  0.0 842.9 jit_solution(13034769948467477972)
XLA Ops:
  8.1 1.8 copy.8
  9.9 14.2 %gather_fusion = f32[4096,64]{1,0:T(8,128)} fusion(f32[64,4096]{0,1:T(8,128)S(1)} %copy.8, s32[4096]{0:T(1024)S(1)} %fusion.8), kind=kCustom, calls=%fused_computation | custom fusion | bytes 2113536 | tf_op jit(solution)/shard_map/jit(_take)/gather | solution.py:46
  24.1 2.2 copy.9
  27.5 30.2 %reduce-scatter.2.cloned.1.call-done = f32[2,64,512]{2,1,0:T(8,128)} async-done(((f32[8,64,512]{2,1,0:T(8,128)}), f32[2,64,512]{2,1,0:T(8,128)}) %reduce-scatter.2.cloned.1.call-update) | async-done | bytes 262160 | tf_op jit(solution)/shard_map/reduce_scatter | solution.py:48
  61.9 6.9 collective-permute-done.1
  72.1 4.2 collective-permute-done.2
  76.4 759.3 %while.16 = (s32[]{:T(128)}, f32[64,4,1,128]{3,1,0,2:T(4,128)S(1)}, s32[]{:T(128)}, f32[2,64,512]{2,1,0:T(8,128)S(1)}, f32[1024,512]{1,0:T(8,128)S(1)}, /*index=...) while((s32[]{:T(128)}, f32[64,4,1,128]{3,1,0,2:T(4,128)S(1)}, ...), condition=%wide.region_4.5_spmd, body=%wide.region_1.4_spmd.sunk | while | flops 402792448 | bytes 4557184 | solution.py:85
  78.4 53.9 %all-reduce.3.cloned.1.call-done = f32[64,512]{1,0:T(8,128)} async-done(((f32[64,512]{1,0:T(8,128)}), f32[64,512]{1,0:T(8,128)}) %all-reduce.3.cloned.1.call-update) | async-done | bytes 131088 | tf_op jit(solution)/shard_map/while/body/eval_jaxpr/psum | solution.py:72
  132.3 3.1 convolution_select_fusion.2
  135.4 34.1 %all-reduce.5.cloned.1.call-done = f32[64,512]{1,0:T(8,128)} async-done(((f32[64,512]{1,0:T(8,128)}), f32[64,512]{1,0:T(8,128)}) %all-reduce.5.cloned.1.call-update) | async-done | bytes 131088 | tf_op jit(solution)/shard_map/while/body/eval_jaxpr/psum | solution.py:17
  172.5 54.8 %all-reduce.3.cloned.1.call-done = f32[64,512]{1,0:T(8,128)} async-done(((f32[64,512]{1,0:T(8,128)}), f32[64,512]{1,0:T(8,128)}) %all-reduce.3.cloned.1.call-update) | async-done | bytes 131088 | tf_op jit(solution)/shard_map/while/body/eval_jaxpr/psum | solution.py:72
  227.3 3.1 convolution_select_fusion.2
  230.4 34.1 %all-reduce.5.cloned.1.call-done = f32[64,512]{1,0:T(8,128)} async-done(((f32[64,512]{1,0:T(8,128)}), f32[64,512]{1,0:T(8,128)}) %all-reduce.5.cloned.1.call-update) | async-done | bytes 131088 | tf_op jit(solution)/shard_map/while/body/eval_jaxpr/psum | solution.py:17
  265.6 1.8 convolution_bitcast_fusion.2
  267.5 54.8 %all-reduce.3.cloned.1.call-done = f32[64,512]{1,0:T(8,128)} async-done(((f32[64,512]{1,0:T(8,128)}), f32[64,512]{1,0:T(8,128)}) %all-reduce.3.cloned.1.call-update) | async-done | bytes 131088 | tf_op jit(solution)/shard_map/while/body/eval_jaxpr/psum | solution.py:72
  322.3 3.1 convolution_select_fusion.2
  325.4 34.1 %all-reduce.5.cloned.1.call-done = f32[64,512]{1,0:T(8,128)} async-done(((f32[64,512]{1,0:T(8,128)}), f32[64,512]{1,0:T(8,128)}) %all-reduce.5.cloned.1.call-update) | async-done | bytes 131088 | tf_op jit(solution)/shard_map/while/body/eval_jaxpr/psum | solution.py:17
  362.5 55.1 %all-reduce.3.cloned.1.call-done = f32[64,512]{1,0:T(8,128)} async-done(((f32[64,512]{1,0:T(8,128)}), f32[64,512]{1,0:T(8,128)}) %all-reduce.3.cloned.1.call-update) | async-done | bytes 131088 | tf_op jit(solution)/shard_map/while/body/eval_jaxpr/psum | solution.py:72
  417.5 3.1 convolution_select_fusion.2
  420.7 34.1 %all-reduce.5.cloned.1.call-done = f32[64,512]{1,0:T(8,128)} async-done(((f32[64,512]{1,0:T(8,128)}), f32[64,512]{1,0:T(8,128)}) %all-reduce.5.cloned.1.call-update) | async-done | bytes 131088 | tf_op jit(solution)/shard_map/while/body/eval_jaxpr/psum | solution.py:17
  457.8 54.8 %all-reduce.3.cloned.1.call-done = f32[64,512]{1,0:T(8,128)} async-done(((f32[64,512]{1,0:T(8,128)}), f32[64,512]{1,0:T(8,128)}) %all-reduce.3.cloned.1.call-update) | async-done | bytes 131088 | tf_op jit(solution)/shard_map/while/body/eval_jaxpr/psum | solution.py:72
  512.5 3.1 convolution_select_fusion.2
  515.7 34.1 %all-reduce.5.cloned.1.call-done = f32[64,512]{1,0:T(8,128)} async-done(((f32[64,512]{1,0:T(8,128)}), f32[64,512]{1,0:T(8,128)}) %all-reduce.5.cloned.1.call-update) | async-done | bytes 131088 | tf_op jit(solution)/shard_map/while/body/eval_jaxpr/psum | solution.py:17
  552.8 54.8 %all-reduce.3.cloned.1.call-done = f32[64,512]{1,0:T(8,128)} async-done(((f32[64,512]{1,0:T(8,128)}), f32[64,512]{1,0:T(8,128)}) %all-reduce.3.cloned.1.call-update) | async-done | bytes 131088 | tf_op jit(solution)/shard_map/while/body/eval_jaxpr/psum | solution.py:72
  607.5 3.1 convolution_select_fusion.2
  610.7 34.1 %all-reduce.5.cloned.1.call-done = f32[64,512]{1,0:T(8,128)} async-done(((f32[64,512]{1,0:T(8,128)}), f32[64,512]{1,0:T(8,128)}) %all-reduce.5.cloned.1.call-update) | async-done | bytes 131088 | tf_op jit(solution)/shard_map/while/body/eval_jaxpr/psum | solution.py:17
  647.7 54.8 %all-reduce.3.cloned.1.call-done = f32[64,512]{1,0:T(8,128)} async-done(((f32[64,512]{1,0:T(8,128)}), f32[64,512]{1,0:T(8,128)}) %all-reduce.3.cloned.1.call-update) | async-done | bytes 131088 | tf_op jit(solution)/shard_map/while/body/eval_jaxpr/psum | solution.py:72
  702.5 3.1 convolution_select_fusion.2
  705.6 34.1 %all-reduce.5.cloned.1.call-done = f32[64,512]{1,0:T(8,128)} async-done(((f32[64,512]{1,0:T(8,128)}), f32[64,512]{1,0:T(8,128)}) %all-reduce.5.cloned.1.call-update) | async-done | bytes 131088 | tf_op jit(solution)/shard_map/while/body/eval_jaxpr/psum | solution.py:17
  742.7 54.8 %all-reduce.3.cloned.1.call-done = f32[64,512]{1,0:T(8,128)} async-done(((f32[64,512]{1,0:T(8,128)}), f32[64,512]{1,0:T(8,128)}) %all-reduce.3.cloned.1.call-update) | async-done | bytes 131088 | tf_op jit(solution)/shard_map/while/body/eval_jaxpr/psum | solution.py:72
  797.5 3.1 convolution_select_fusion.2
  800.6 34.1 %all-reduce.5.cloned.1.call-done = f32[64,512]{1,0:T(8,128)} async-done(((f32[64,512]{1,0:T(8,128)}), f32[64,512]{1,0:T(8,128)}) %all-reduce.5.cloned.1.call-update) | async-done | bytes 131088 | tf_op jit(solution)/shard_map/while/body/eval_jaxpr/psum | solution.py:17
  (81 shorter events, 32.4 us)
Async XLA Ops:
  6.5 51.1 %reduce-scatter.2.cloned.1.call-start = ((), (), s32[]{:S(2)}) async-start(), calls=%async_computation.1 | async-start | bytes 1310720 | tf_op jit(solution)/shard_map/reduce_scatter | solution.py:48
  57.6 1.7 collective-permute-start
  60.4 8.4 collective-permute-start.1
  68.8 7.6 collective-permute-start.2
  76.4 55.8 %all-reduce.3.cloned.1.call-start = ((), (), s32[]{:S(2)}) async-start(), calls=%async_computation.2 | async-start | bytes 262144 | tf_op jit(solution)/shard_map/while/body/eval_jaxpr/psum | solution.py:72
  78.3 91.2 %all-reduce.5.cloned.1.call-start = ((), (), s32[]{:S(2)}) async-start(), calls=%async_computation.3 | async-start | bytes 262144 | tf_op jit(solution)/shard_map/while/body/eval_jaxpr/psum | solution.py:17
  170.6 56.7 %all-reduce.3.cloned.1.call-start = ((), (), s32[]{:S(2)}) async-start(), calls=%async_computation.2 | async-start | bytes 262144 | tf_op jit(solution)/shard_map/while/body/eval_jaxpr/psum | solution.py:72
  172.4 92.1 %all-reduce.5.cloned.1.call-start = ((), (), s32[]{:S(2)}) async-start(), calls=%async_computation.3 | async-start | bytes 262144 | tf_op jit(solution)/shard_map/while/body/eval_jaxpr/psum | solution.py:17
  265.5 56.7 %all-reduce.3.cloned.1.call-start = ((), (), s32[]{:S(2)}) async-start(), calls=%async_computation.2 | async-start | bytes 262144 | tf_op jit(solution)/shard_map/while/body/eval_jaxpr/psum | solution.py:72
  267.4 92.1 %all-reduce.5.cloned.1.call-start = ((), (), s32[]{:S(2)}) async-start(), calls=%async_computation.3 | async-start | bytes 262144 | tf_op jit(solution)/shard_map/while/body/eval_jaxpr/psum | solution.py:17
  360.5 57.0 %all-reduce.3.cloned.1.call-start = ((), (), s32[]{:S(2)}) async-start(), calls=%async_computation.2 | async-start | bytes 262144 | tf_op jit(solution)/shard_map/while/body/eval_jaxpr/psum | solution.py:72
  362.4 92.4 %all-reduce.5.cloned.1.call-start = ((), (), s32[]{:S(2)}) async-start(), calls=%async_computation.3 | async-start | bytes 262144 | tf_op jit(solution)/shard_map/while/body/eval_jaxpr/psum | solution.py:17
  455.8 56.7 %all-reduce.3.cloned.1.call-start = ((), (), s32[]{:S(2)}) async-start(), calls=%async_computation.2 | async-start | bytes 262144 | tf_op jit(solution)/shard_map/while/body/eval_jaxpr/psum | solution.py:72
  457.7 92.1 %all-reduce.5.cloned.1.call-start = ((), (), s32[]{:S(2)}) async-start(), calls=%async_computation.3 | async-start | bytes 262144 | tf_op jit(solution)/shard_map/while/body/eval_jaxpr/psum | solution.py:17
  550.8 56.7 %all-reduce.3.cloned.1.call-start = ((), (), s32[]{:S(2)}) async-start(), calls=%async_computation.2 | async-start | bytes 262144 | tf_op jit(solution)/shard_map/while/body/eval_jaxpr/psum | solution.py:72
  552.7 92.1 %all-reduce.5.cloned.1.call-start = ((), (), s32[]{:S(2)}) async-start(), calls=%async_computation.3 | async-start | bytes 262144 | tf_op jit(solution)/shard_map/while/body/eval_jaxpr/psum | solution.py:17
  645.8 56.7 %all-reduce.3.cloned.1.call-start = ((), (), s32[]{:S(2)}) async-start(), calls=%async_computation.2 | async-start | bytes 262144 | tf_op jit(solution)/shard_map/while/body/eval_jaxpr/psum | solution.py:72
  647.7 92.1 %all-reduce.5.cloned.1.call-start = ((), (), s32[]{:S(2)}) async-start(), calls=%async_computation.3 | async-start | bytes 262144 | tf_op jit(solution)/shard_map/while/body/eval_jaxpr/psum | solution.py:17
  740.8 56.7 %all-reduce.3.cloned.1.call-start = ((), (), s32[]{:S(2)}) async-start(), calls=%async_computation.2 | async-start | bytes 262144 | tf_op jit(solution)/shard_map/while/body/eval_jaxpr/psum | solution.py:72
  742.7 92.1 %all-reduce.5.cloned.1.call-start = ((), (), s32[]{:S(2)}) async-start(), calls=%async_computation.3 | async-start | bytes 262144 | tf_op jit(solution)/shard_map/while/body/eval_jaxpr/psum | solution.py:17
  835.7 0.7 copy-start
Sparse Core Ops, SparseCore 0:
  27.6 29.9 reduce-scatter.1
  80.3 51.9 all-reduce.2
  135.5 34.0 all-reduce.4
  174.1 53.1 all-reduce.2
  230.5 34.0 all-reduce.4
  269.1 53.1 all-reduce.2
  325.5 34.0 all-reduce.4
  364.4 53.1 all-reduce.2
  420.8 34.0 all-reduce.4
  459.4 53.1 all-reduce.2
  515.7 34.0 all-reduce.4
  554.3 53.1 all-reduce.2
  610.7 34.0 all-reduce.4
  649.3 53.1 all-reduce.2
  705.7 34.0 all-reduce.4
  744.3 53.1 all-reduce.2
  800.7 34.0 all-reduce.4
